TPU v7x, 32 devices: a whole 2x2x4 slice. The times are simulated.
32 devices in a mesh: seq: 8 (over z, y), fsdp: 4 (over x, core).
Axes of the slice: x: 2, y: 2, z: 4, core: 2. Of those that a mesh axis runs over, the one named last changes fastest.
Arguments:
- queries: bfloat16 [1024, 2048], P('seq', 'fsdp'), may hold values from -260 to 260
- layer_input: bfloat16 [1024, 4096], P('seq'), may hold values from -6 to 6
- w_key: bfloat16 [4096, 512], P('seq', 'fsdp'), may hold values from -0.09375 to 0.09375
- w_value: bfloat16 [4096, 512], P('seq', 'fsdp'), may hold values from -0.09375 to 0.09375
- grad_out: bfloat16 [1024, 2048], P('seq', 'fsdp'), may hold values from -6 to 6
Outputs:
- attn_out: bfloat16 [1024, 2048], P('seq', 'fsdp')
- grad_queries: bfloat16 [1024, 2048], P('seq', 'fsdp')
- grad_input: bfloat16 [1024, 4096], P('seq', 'fsdp')
- grad_w_key: float32 [4096, 512], P('seq', 'fsdp')
- grad_w_value: float32 [4096, 512], P('seq', 'fsdp')
All inputs are finite; a program needn't handle non-finite values.
Results may differ from a plain program's by a relative error of at most 0.04.
Values may be sent and summed in bfloat16 or wider, within the bound.
A program may use at most 64 MiB of HBM per device.

v0:
```python
import jax
import jax.numpy as jnp
from jax import lax
from jax.sharding import PartitionSpec as P

HD = 128


ROPE_BASE = 500000.0
NEG = -1e30


def passed_along(block, axis, distance):
    devices = range(lax.axis_size(axis))
    route = [((i - distance) % len(devices), i) for i in devices]
    return lax.ppermute(block, axis, route)


def rope_tables(positions, half):
    freq = ROPE_BASE ** (-(jnp.arange(half, dtype=jnp.float32) * (2.0 / (2 * half))))
    angle = positions.astype(jnp.float32)[:, None] * freq[None, :]
    return (jnp.cos(angle), jnp.sin(angle))


def rotate(heads, cosine, sine):
    half = heads.shape[-1] // 2
    first = heads[..., :half]
    second = heads[..., half:]
    cos_b = cosine[:, None, :]
    sin_b = sine[:, None, :]
    return jnp.concatenate(
        [first * cos_b - second * sin_b, second * cos_b + first * sin_b], axis=-1
    )


def masked_scores(query, key_blk, start, first_query):
    scores = jnp.einsum(
        "qhgd,khd->hgqk", query, key_blk, preferred_element_type=jnp.float32
    ) * HD ** (-0.5)
    query_pos = first_query + jnp.arange(query.shape[0], dtype=jnp.int32)
    key_pos = start + jnp.arange(key_blk.shape[0], dtype=jnp.int32)
    mask = key_pos[None, :] <= query_pos[:, None]
    return (jnp.where(mask, scores, NEG), mask)


def forward_piece(state, query, key_blk, value_blk, start, first_query):
    running_max, running_sum, weighted = state
    scores, mask = masked_scores(query, key_blk, start, first_query)
    new_max = jnp.maximum(running_max, jnp.max(scores, axis=-1))
    expo = jnp.where(mask, jnp.exp(scores - new_max[..., None]), 0.0)
    new_sum = jnp.sum(expo, axis=-1)
    moved = jnp.einsum(
        "hgqk,khd->qhgd", expo.astype(jnp.bfloat16), value_blk, preferred_element_type=jnp.float32
    )
    weighted = moved
    return (new_max, new_sum, weighted)


def backward_piece(query, upstream, lse, delta, key_blk, value_blk, start, first_query):
    scores, mask = masked_scores(query, key_blk, start, first_query)
    probs = jnp.where(mask, jnp.exp(scores - lse[..., None]), 0.0)
    dprobs = jnp.einsum("qhgd,khd->hgqk", upstream, value_blk, preferred_element_type=jnp.float32)
    dscores = probs * (dprobs - delta[..., None])
    value_term = jnp.einsum(
        "hgqk,qhgd->khd", probs.astype(jnp.bfloat16), upstream, preferred_element_type=jnp.float32
    )
    ds_low = dscores.astype(jnp.bfloat16)
    query_term = jnp.einsum("hgqk,khd->qhgd", ds_low, key_blk, preferred_element_type=jnp.float32)
    key_term = jnp.einsum("hgqk,qhgd->khd", ds_low, query, preferred_element_type=jnp.float32)
    return (query_term, key_term, value_term)


def body(queries, layer_input, w_key, w_value, grad_out):
    tok_rows = layer_input.shape[0]
    kv_cols = w_key.shape[1]
    local_heads = kv_cols // HD
    group = queries.shape[1] // kv_cols
    my_block = lax.axis_index("seq")
    seq_count = lax.axis_size("seq")
    first_query = my_block * tok_rows
    scale = HD ** (-0.5)
    full_key, full_value = (
        lax.all_gather(w_key, "seq", axis=0, tiled=True),
        lax.all_gather(w_value, "seq", axis=0, tiled=True),
    )
    key_linear = jnp.dot(layer_input, full_key, preferred_element_type=jnp.float32)
    value_lin = jnp.dot(layer_input, full_value, preferred_element_type=jnp.float32)
    positions = first_query + jnp.arange(tok_rows, dtype=jnp.int32)
    cosine, sine = rope_tables(positions, HD // 2)
    keys = rotate(key_linear.reshape(tok_rows, local_heads, HD), cosine, sine).astype(jnp.bfloat16)
    values = value_lin.reshape(tok_rows, local_heads, HD).astype(jnp.bfloat16)
    row_sets = (queries, grad_out, first_query)
    query_sets = []
    rows, grads, begin = row_sets
    count = rows.shape[0]
    query_sets.append(
        (
            rows.reshape(count, local_heads, group, HD),
            grads.reshape(count, local_heads, group, HD),
            begin,
            begin + count - 1,
        )
    )
    start_state = tuple(
        (
            (
                jnp.full((local_heads, group, qs[0].shape[0]), NEG, jnp.float32),
                jnp.zeros((local_heads, group, qs[0].shape[0]), jnp.float32),
                jnp.zeros((qs[0].shape[0], local_heads, group, HD), jnp.float32),
            )
            for qs in query_sets
        )
    )

    def fold_keys(state, pieces, start):
        results = []
        for member, qs in zip(state, query_sets):

            def apply_fold(member=member, qs=qs):
                return forward_piece(member, qs[0], pieces[0], pieces[1], start, qs[2])

            results.append(lax.cond(start <= qs[3], apply_fold, lambda member=member: member))
        return tuple(results)

    states = fold_keys(
        start_state,
        (
            lax.all_gather(keys, "seq", axis=0, tiled=True),
            lax.all_gather(values, "seq", axis=0, tiled=True),
        ),
        jnp.int32(0),
    )
    finals = []
    for (running_max, running_sum, weighted), qs in zip(states, query_sets):
        output = weighted / jnp.transpose(running_sum, (2, 0, 1))[..., None]
        lse = running_max + jnp.log(running_sum)
        delta = jnp.transpose(jnp.sum(qs[1].astype(jnp.float32) * output, axis=-1), (1, 2, 0))
        finals.append((lse, delta, output.reshape(qs[0].shape[0], -1).astype(jnp.bfloat16)))
    query_zero = tuple(
        (jnp.zeros((qs[0].shape[0], local_heads, group, HD), jnp.float32) for qs in query_sets)
    )

    def add_block(key_blk, value_blk, start, query_accs):
        key_sum = jnp.zeros((key_blk.shape[0], local_heads, HD), jnp.float32)
        value_sum = jnp.zeros((key_blk.shape[0], local_heads, HD), jnp.float32)
        new_accs = []
        for acc, qs, fin in zip(query_accs, query_sets, finals):

            def apply_block(acc=acc, qs=qs, fin=fin, key_sum=key_sum, value_sum=value_sum):
                query_term, key_term, value_term = backward_piece(
                    qs[0], qs[1], fin[0], fin[1], key_blk, value_blk, start, qs[2]
                )
                return (acc + query_term, key_term, value_term)

            def leave_block(acc=acc, key_sum=key_sum, value_sum=value_sum):
                return (acc, key_sum, value_sum)

            acc, key_sum, value_sum = lax.cond(start <= qs[3], apply_block, leave_block)
            new_accs.append(acc)
        return (tuple(new_accs), key_sum, value_sum)

    own_zero = jnp.zeros((tok_rows, local_heads, HD), jnp.float32)

    def pass_keys(key_blk, value_blk):
        return passed_along((key_blk, value_blk), "seq", -1)

    def pass_grads(key_acc, value_acc):
        return passed_along((key_acc, value_acc), "seq", -1)

    def visit(step, key_blk, value_blk, query_accs, key_acc, value_acc):
        start = (my_block + step) % seq_count * tok_rows
        query_accs, key_sum, value_sum = add_block(key_blk, value_blk, start, query_accs)
        return (query_accs, key_acc + key_sum, value_acc + value_sum)

    def cycle_loop(step, carry):
        key_blk, value_blk, query_accs, key_acc, value_acc = carry
        query_accs, key_acc, value_acc = visit(
            step, key_blk, value_blk, query_accs, key_acc, value_acc
        )
        key_acc, value_acc = pass_grads(key_acc, value_acc)
        key_blk, value_blk = pass_keys(key_blk, value_blk)
        return (key_blk, value_blk, query_accs, key_acc, value_acc)

    key_blk, value_blk, query_accs, key_acc, value_acc = lax.fori_loop(
        0, seq_count - 1, cycle_loop, (keys, values, query_zero, own_zero, own_zero)
    )
    query_accs, key_acc, value_acc = visit(
        seq_count - 1, key_blk, value_blk, query_accs, key_acc, value_acc
    )
    key_grad, value_grad = pass_grads(key_acc, value_acc)
    query_outs = [
        (acc * scale).reshape(acc.shape[0], -1).astype(jnp.bfloat16) for acc in query_accs
    ]
    attn_out = finals[0][2]
    grad_queries = query_outs[0]
    key_back = (
        rotate(key_grad * scale, cosine, -sine).astype(jnp.bfloat16).reshape(tok_rows, kv_cols)
    )
    value_back = value_grad.astype(jnp.bfloat16).reshape(tok_rows, kv_cols)
    both_grads = jnp.concatenate([key_back, value_back], axis=1)
    summed = lax.psum_scatter(
        lax.dot_general(
            layer_input, both_grads, (((0,), (0,)), ((), ())), preferred_element_type=jnp.float32
        ),
        "seq",
        scatter_dimension=0,
        tiled=True,
    )
    grad_w_key = summed[:, :kv_cols]
    grad_w_value = summed[:, kv_cols:]
    contract = (((1,), (1,)), ((), ()))
    partial_input = lax.dot_general(
        key_back, full_key, contract, preferred_element_type=jnp.float32
    ) + lax.dot_general(value_back, full_value, contract, preferred_element_type=jnp.float32)
    grad_input = lax.psum_scatter(partial_input, "fsdp", scatter_dimension=1, tiled=True).astype(
        jnp.bfloat16
    )
    return (attn_out, grad_queries, grad_input, grad_w_key, grad_w_value)


def solution(mesh):
    placed = (
        P("seq", "fsdp"),
        P("seq", None),
        P("seq", "fsdp"),
        P("seq", "fsdp"),
        P("seq", "fsdp"),
    )
    return jax.shard_map(
        body,
        mesh=mesh,
        in_specs=placed,
        out_specs=(
            P("seq", "fsdp"),
            P("seq", "fsdp"),
            P("seq", "fsdp"),
            P("seq", "fsdp"),
            P("seq", "fsdp"),
        ),
        check_vma=False,
    )
```

profile of v0, /device:TPU:0, one launch (start us, length us, event | category | flops | bytes accessed | tf_op | source)
XLA Modules:
  0.0 344.3 jit_solution(8674900460732019217)
XLA Ops:
  11.1 42.0 %all-gather.4.cloned.1.call-done = bf16[4096,128]{1,0:T(8,128)(2,1)} async-done(((bf16[512,128]{1,0:T(8,128)(2,1)}), bf16[4096,128]{1,0:T(8,128)(2,1)}) %all-gather.4.cloned.1.call-update) | async-done | bytes 1048592 | tf_op jit(solution)/shard_map/all_gather | solution.py:83
  53.2 1.7 convolution_bitcast_fusion.10
  55.2 26.8 %all_gather.13 = bf16[1024,1,128]{0,2,1:T(8,128)(2,1)S(1)} all-gather(bf16[128,1,128]{0,2,1:T(8,128)(2,1)S(1)} %pad_maximum_fusion), channel_id=1, replica_groups=mesh['seq'=8,'fsdp'=4] {'seq'}, dimensions={0}, use_global_device_ids=true | all-gather | bytes 294912 | tf_op jit(solution)/shard_map/all_gather | solution.py:128
  82.0 13.2 %all-gather.6.cloned.1.call-done = bf16[4096,128]{1,0:T(8,128)(2,1)} async-done(((bf16[512,128]{1,0:T(8,128)(2,1)}), bf16[4096,128]{1,0:T(8,128)(2,1)}) %all-gather.6.cloned.1.call-update) | async-done | bytes 1048592 | tf_op jit(solution)/shard_map/all_gather | solution.py:84
  95.2 1.6 convolution_convert_fusion
  96.8 30.8 %all-gather = bf16[1024,128]{1,0:T(8,128)(2,1)S(1)} all-gather(bf16[128,128]{1,0:T(8,128)(2,1)S(1)} %convolution_convert_fusion), channel_id=2, replica_groups=mesh['seq'=8,'fsdp'=4] {'seq'}, dimensions={0}, use_global_device_ids=true | all-gather | bytes 294912 | tf_op jit(solution)/shard_map/all_gather | solution.py:129
  127.6 3.3 conditional.3
  131.7 68.9 %while.29 = (s32[]{:T(128)}, bf16[128,1,128]{2,0,1:T(8,128)(2,1)S(1)}, bf16[128,1,128]{2,0,1:T(8,128)(2,1)S(1)}, f32[128,1,4,128]{3,0,2,1:T(8,128)S(1)}, f32[128...) while((s32[]{:T(128)}, ...), condition=%wide.region_8.9_spmd, body=%wide.region_5.8_spmd.sunk | while | flops 84525328 | bytes 3807808 | solution.py:184
  133.0 2.0 collective-permute-start.2
  135.3 4.6 %collective-permute-done = bf16[128,1,128]{2,0,1:T(8,128)(2,1)S(1)} collective-permute-done((bf16[128,1,128]{2,0,1:T(8,128)(2,1)S(1)}, bf16[128,1,128]{2,0,1:T(8,128)(2,1)S(1)}, u32[]{:S(2)}, u32[]{:S(2)}) %collective-permute-start) | collective-permute-done | bytes 32800 | tf_op jit(solution)/shard_map/while/body/eval_jaxpr/ppermute | solution.py:16
  140.4 5.5 %collective-permute-start.2 = (f32[128,1,128]{2,0,1:T(8,128)S(1)}, f32[128,1,128]{2,0,1:T(8,128)S(1)}, u32[]{:S(2)}, u32[]{:S(2)}) collective-permute-start(f32[128,1,128]{2,0,1:T(8,128)S(1)} %add.200), channel_id=1, source_target_pairs={{4,0},{8,4},{12,8},{16,12},{20,16},{24,20},{28,24},{0,28},{5,1},{9... | collective-permute-start | bytes 196616 | tf_op jit(solution)/shard_map/while/body/eval_jaxpr/ppermute | solution.py:16
  146.1 4.5 %collective-permute-done = bf16[128,1,128]{2,0,1:T(8,128)(2,1)S(1)} collective-permute-done((bf16[128,1,128]{2,0,1:T(8,128)(2,1)S(1)}, bf16[128,1,128]{2,0,1:T(8,128)(2,1)S(1)}, u32[]{:S(2)}, u32[]{:S(2)}) %collective-permute-start) | collective-permute-done | bytes 32800 | tf_op jit(solution)/shard_map/while/body/eval_jaxpr/ppermute | solution.py:16
  151.0 4.8 %collective-permute-start.2 = (f32[128,1,128]{2,0,1:T(8,128)S(1)}, f32[128,1,128]{2,0,1:T(8,128)S(1)}, u32[]{:S(2)}, u32[]{:S(2)}) collective-permute-start(f32[128,1,128]{2,0,1:T(8,128)S(1)} %add.200), channel_id=1, source_target_pairs={{4,0},{8,4},{12,8},{16,12},{20,16},{24,20},{28,24},{0,28},{5,1},{9... | collective-permute-start | bytes 196616 | tf_op jit(solution)/shard_map/while/body/eval_jaxpr/ppermute | solution.py:16
  156.0 4.5 %collective-permute-done = bf16[128,1,128]{2,0,1:T(8,128)(2,1)S(1)} collective-permute-done((bf16[128,1,128]{2,0,1:T(8,128)(2,1)S(1)}, bf16[128,1,128]{2,0,1:T(8,128)(2,1)S(1)}, u32[]{:S(2)}, u32[]{:S(2)}) %collective-permute-start) | collective-permute-done | bytes 32800 | tf_op jit(solution)/shard_map/while/body/eval_jaxpr/ppermute | solution.py:16
  161.1 4.4 %collective-permute-start.2 = (f32[128,1,128]{2,0,1:T(8,128)S(1)}, f32[128,1,128]{2,0,1:T(8,128)S(1)}, u32[]{:S(2)}, u32[]{:S(2)}) collective-permute-start(f32[128,1,128]{2,0,1:T(8,128)S(1)} %add.200), channel_id=1, source_target_pairs={{4,0},{8,4},{12,8},{16,12},{20,16},{24,20},{28,24},{0,28},{5,1},{9... | collective-permute-start | bytes 196616 | tf_op jit(solution)/shard_map/while/body/eval_jaxpr/ppermute | solution.py:16
  165.5 1.4 collective-permute-start
  167.1 3.1 collective-permute-done
  171.4 3.8 %collective-permute-start.2 = (f32[128,1,128]{2,0,1:T(8,128)S(1)}, f32[128,1,128]{2,0,1:T(8,128)S(1)}, u32[]{:S(2)}, u32[]{:S(2)}) collective-permute-start(f32[128,1,128]{2,0,1:T(8,128)S(1)} %add.200), channel_id=1, source_target_pairs={{4,0},{8,4},{12,8},{16,12},{20,16},{24,20},{28,24},{0,28},{5,1},{9... | collective-permute-start | bytes 196616 | tf_op jit(solution)/shard_map/while/body/eval_jaxpr/ppermute | solution.py:16
  175.3 1.9 collective-permute-start
  177.6 2.3 collective-permute-done
  181.2 4.2 %collective-permute-start.2 = (f32[128,1,128]{2,0,1:T(8,128)S(1)}, f32[128,1,128]{2,0,1:T(8,128)S(1)}, u32[]{:S(2)}, u32[]{:S(2)}) collective-permute-start(f32[128,1,128]{2,0,1:T(8,128)S(1)} %add.200), channel_id=1, source_target_pairs={{4,0},{8,4},{12,8},{16,12},{20,16},{24,20},{28,24},{0,28},{5,1},{9... | collective-permute-start | bytes 196616 | tf_op jit(solution)/shard_map/while/body/eval_jaxpr/ppermute | solution.py:16
  185.5 1.4 collective-permute-start
  187.0 3.1 collective-permute-done
  191.3 4.3 %collective-permute-start.2 = (f32[128,1,128]{2,0,1:T(8,128)S(1)}, f32[128,1,128]{2,0,1:T(8,128)S(1)}, u32[]{:S(2)}, u32[]{:S(2)}) collective-permute-start(f32[128,1,128]{2,0,1:T(8,128)S(1)} %add.200), channel_id=1, source_target_pairs={{4,0},{8,4},{12,8},{16,12},{20,16},{24,20},{28,24},{0,28},{5,1},{9... | collective-permute-start | bytes 196616 | tf_op jit(solution)/shard_map/while/body/eval_jaxpr/ppermute | solution.py:16
  197.0 3.3 collective-permute-done
  200.8 4.5 %collective-permute-start.4 = (f32[128,1,128]{0,2,1:T(8,128)S(1)}, f32[128,1,128]{0,2,1:T(8,128)S(1)}, u32[]{:S(2)}, u32[]{:S(2)}) collective-permute-start(f32[128,1,128]{0,2,1:T(8,128)S(1)} %add.165), channel_id=1, source_target_pairs={{4,0},{8,4},{12,8},{16,12},{20,16},{24,20},{28,24},{0,28},{5,1},{9... | collective-permute-start | bytes 196616 | tf_op jit(solution)/shard_map/ppermute | solution.py:16
  205.4 1.8 collective-permute-done.4
  209.3 1.8 convolution_add_fusion
  211.4 2.8 convolution_bitcast_fusion.9
  215.8 27.0 %reduce-scatter.3.cloned.1.call-done = f32[128,1024]{1,0:T(8,128)} async-done(((f32[128,4096]{1,0:T(8,128)}), f32[128,1024]{1,0:T(8,128)}) %reduce-scatter.3.cloned.1.call-update) | async-done | bytes 524304 | tf_op jit(solution)/shard_map/reduce_scatter | solution.py:215
  242.8 1.8 convert_element_type.97
  244.6 90.4 %reduce-scatter.5.cloned.1.call-done = f32[512,256]{0,1:T(8,128)} async-done(((f32[4096,256]{0,1:T(8,128)}), f32[512,256]{0,1:T(8,128)}) %reduce-scatter.5.cloned.1.call-update) | async-done | bytes 524304 | tf_op jit(solution)/shard_map/reduce_scatter | solution.py:201
  (149 shorter events, 25.6 us)
Async XLA Ops:
  7.2 46.0 %all-gather.4.cloned.1.call-start = ((), (), s32[]{:S(2)}) async-start(), calls=%async_computation.2 | async-start | bytes 1179648 | tf_op jit(solution)/shard_map/all_gather | solution.py:83
  7.9 87.3 %all-gather.6.cloned.1.call-start = ((), (), s32[]{:S(2)}) async-start(), calls=%async_computation.3 | async-start | bytes 1179648 | tf_op jit(solution)/shard_map/all_gather | solution.py:84
  8.7 234.2 %reduce-scatter.3.cloned.1.call-start = ((), (), s32[]{:S(2)}) async-start(), calls=%async_computation.4 | async-start | bytes 2621440 | tf_op jit(solution)/shard_map/reduce_scatter | solution.py:215
  133.0 7.3 %collective-permute-start.2 = (f32[128,1,128]{2,0,1:T(8,128)S(1)}, f32[128,1,128]{2,0,1:T(8,128)S(1)}, u32[]{:S(2)}, u32[]{:S(2)}) collective-permute-start(f32[128,1,128]{2,0,1:T(8,128)S(1)} %add.200), channel_id=1, source_target_pairs={{4,0},{8,4},{12,8},{16,12},{20,16},{24,20},{28,24},{0,28},{5,1},{9... | collective-permute-start | bytes 196616 | tf_op jit(solution)/shard_map/while/body/eval_jaxpr/ppermute | solution.py:16
  135.0 5.3 %collective-permute-start.3 = (f32[128,1,128]{2,0,1:T(8,128)S(1)}, f32[128,1,128]{2,0,1:T(8,128)S(1)}, u32[]{:S(2)}, u32[]{:S(2)}) collective-permute-start(f32[128,1,128]{2,0,1:T(8,128)S(1)} %add.201), channel_id=1, source_target_pairs={{4,0},{8,4},{12,8},{16,12},{20,16},{24,20},{28,24},{0,28},{5,1},{9... | collective-permute-start | bytes 196616 | tf_op jit(solution)/shard_map/while/body/eval_jaxpr/ppermute | solution.py:16
  135.1 4.8 %collective-permute-start = (bf16[128,1,128]{2,0,1:T(8,128)(2,1)S(1)}, bf16[128,1,128]{2,0,1:T(8,128)(2,1)S(1)}, u32[]{:S(2)}, u32[]{:S(2)}) collective-permute-start(bf16[128,1,128]{2,0,1:T(8,128)(2,1)S(1)} %copy.75), channel_id=1, source_target_pairs={{4,0},{8,4},{12,8},{16,12},{20,16},{24,20},{28,24},{0,28},{5,1},{9... | collective-permute-start | bytes 98312 | tf_op jit(solution)/shard_map/while/body/eval_jaxpr/ppermute | solution.py:16
  135.3 5.0 %collective-permute-start.1 = (bf16[128,1,128]{2,0,1:T(8,128)(2,1)S(1)}, bf16[128,1,128]{2,0,1:T(8,128)(2,1)S(1)}, u32[]{:S(2)}, u32[]{:S(2)}) collective-permute-start(bf16[128,1,128]{2,0,1:T(8,128)(2,1)S(1)} %copy.76), channel_id=1, source_target_pairs={{4,0},{8,4},{12,8},{16,12},{20,16},{24,20},{28,24},{0,28},{5,1},{9... | collective-permute-start | bytes 98312 | tf_op jit(solution)/shard_map/while/body/eval_jaxpr/ppermute | solution.py:16
  140.4 10.5 %collective-permute-start.2 = (f32[128,1,128]{2,0,1:T(8,128)S(1)}, f32[128,1,128]{2,0,1:T(8,128)S(1)}, u32[]{:S(2)}, u32[]{:S(2)}) collective-permute-start(f32[128,1,128]{2,0,1:T(8,128)S(1)} %add.200), channel_id=1, source_target_pairs={{4,0},{8,4},{12,8},{16,12},{20,16},{24,20},{28,24},{0,28},{5,1},{9... | collective-permute-start | bytes 196616 | tf_op jit(solution)/shard_map/while/body/eval_jaxpr/ppermute | solution.py:16
  145.8 5.0 %collective-permute-start.3 = (f32[128,1,128]{2,0,1:T(8,128)S(1)}, f32[128,1,128]{2,0,1:T(8,128)S(1)}, u32[]{:S(2)}, u32[]{:S(2)}) collective-permute-start(f32[128,1,128]{2,0,1:T(8,128)S(1)} %add.201), channel_id=1, source_target_pairs={{4,0},{8,4},{12,8},{16,12},{20,16},{24,20},{28,24},{0,28},{5,1},{9... | collective-permute-start | bytes 196616 | tf_op jit(solution)/shard_map/while/body/eval_jaxpr/ppermute | solution.py:16
  145.9 4.6 %collective-permute-start = (bf16[128,1,128]{2,0,1:T(8,128)(2,1)S(1)}, bf16[128,1,128]{2,0,1:T(8,128)(2,1)S(1)}, u32[]{:S(2)}, u32[]{:S(2)}) collective-permute-start(bf16[128,1,128]{2,0,1:T(8,128)(2,1)S(1)} %copy.75), channel_id=1, source_target_pairs={{4,0},{8,4},{12,8},{16,12},{20,16},{24,20},{28,24},{0,28},{5,1},{9... | collective-permute-start | bytes 98312 | tf_op jit(solution)/shard_map/while/body/eval_jaxpr/ppermute | solution.py:16
  146.0 4.9 %collective-permute-start.1 = (bf16[128,1,128]{2,0,1:T(8,128)(2,1)S(1)}, bf16[128,1,128]{2,0,1:T(8,128)(2,1)S(1)}, u32[]{:S(2)}, u32[]{:S(2)}) collective-permute-start(bf16[128,1,128]{2,0,1:T(8,128)(2,1)S(1)} %copy.76), channel_id=1, source_target_pairs={{4,0},{8,4},{12,8},{16,12},{20,16},{24,20},{28,24},{0,28},{5,1},{9... | collective-permute-start | bytes 98312 | tf_op jit(solution)/shard_map/while/body/eval_jaxpr/ppermute | solution.py:16
  151.0 10.0 %collective-permute-start.2 = (f32[128,1,128]{2,0,1:T(8,128)S(1)}, f32[128,1,128]{2,0,1:T(8,128)S(1)}, u32[]{:S(2)}, u32[]{:S(2)}) collective-permute-start(f32[128,1,128]{2,0,1:T(8,128)S(1)} %add.200), channel_id=1, source_target_pairs={{4,0},{8,4},{12,8},{16,12},{20,16},{24,20},{28,24},{0,28},{5,1},{9... | collective-permute-start | bytes 196616 | tf_op jit(solution)/shard_map/while/body/eval_jaxpr/ppermute | solution.py:16
  155.8 5.1 %collective-permute-start.3 = (f32[128,1,128]{2,0,1:T(8,128)S(1)}, f32[128,1,128]{2,0,1:T(8,128)S(1)}, u32[]{:S(2)}, u32[]{:S(2)}) collective-permute-start(f32[128,1,128]{2,0,1:T(8,128)S(1)} %add.201), channel_id=1, source_target_pairs={{4,0},{8,4},{12,8},{16,12},{20,16},{24,20},{28,24},{0,28},{5,1},{9... | collective-permute-start | bytes 196616 | tf_op jit(solution)/shard_map/while/body/eval_jaxpr/ppermute | solution.py:16
  155.9 4.6 %collective-permute-start = (bf16[128,1,128]{2,0,1:T(8,128)(2,1)S(1)}, bf16[128,1,128]{2,0,1:T(8,128)(2,1)S(1)}, u32[]{:S(2)}, u32[]{:S(2)}) collective-permute-start(bf16[128,1,128]{2,0,1:T(8,128)(2,1)S(1)} %copy.75), channel_id=1, source_target_pairs={{4,0},{8,4},{12,8},{16,12},{20,16},{24,20},{28,24},{0,28},{5,1},{9... | collective-permute-start | bytes 98312 | tf_op jit(solution)/shard_map/while/body/eval_jaxpr/ppermute | solution.py:16
  156.0 5.0 %collective-permute-start.1 = (bf16[128,1,128]{2,0,1:T(8,128)(2,1)S(1)}, bf16[128,1,128]{2,0,1:T(8,128)(2,1)S(1)}, u32[]{:S(2)}, u32[]{:S(2)}) collective-permute-start(bf16[128,1,128]{2,0,1:T(8,128)(2,1)S(1)} %copy.76), channel_id=1, source_target_pairs={{4,0},{8,4},{12,8},{16,12},{20,16},{24,20},{28,24},{0,28},{5,1},{9... | collective-permute-start | bytes 98312 | tf_op jit(solution)/shard_map/while/body/eval_jaxpr/ppermute | solution.py:16
  161.1 10.2 %collective-permute-start.2 = (f32[128,1,128]{2,0,1:T(8,128)S(1)}, f32[128,1,128]{2,0,1:T(8,128)S(1)}, u32[]{:S(2)}, u32[]{:S(2)}) collective-permute-start(f32[128,1,128]{2,0,1:T(8,128)S(1)} %add.200), channel_id=1, source_target_pairs={{4,0},{8,4},{12,8},{16,12},{20,16},{24,20},{28,24},{0,28},{5,1},{9... | collective-permute-start | bytes 196616 | tf_op jit(solution)/shard_map/while/body/eval_jaxpr/ppermute | solution.py:16
  165.5 5.8 %collective-permute-start.3 = (f32[128,1,128]{2,0,1:T(8,128)S(1)}, f32[128,1,128]{2,0,1:T(8,128)S(1)}, u32[]{:S(2)}, u32[]{:S(2)}) collective-permute-start(f32[128,1,128]{2,0,1:T(8,128)S(1)} %add.201), channel_id=1, source_target_pairs={{4,0},{8,4},{12,8},{16,12},{20,16},{24,20},{28,24},{0,28},{5,1},{9... | collective-permute-start | bytes 196616 | tf_op jit(solution)/shard_map/while/body/eval_jaxpr/ppermute | solution.py:16
  165.5 4.6 %collective-permute-start = (bf16[128,1,128]{2,0,1:T(8,128)(2,1)S(1)}, bf16[128,1,128]{2,0,1:T(8,128)(2,1)S(1)}, u32[]{:S(2)}, u32[]{:S(2)}) collective-permute-start(bf16[128,1,128]{2,0,1:T(8,128)(2,1)S(1)} %copy.75), channel_id=1, source_target_pairs={{4,0},{8,4},{12,8},{16,12},{20,16},{24,20},{28,24},{0,28},{5,1},{9... | collective-permute-start | bytes 98312 | tf_op jit(solution)/shard_map/while/body/eval_jaxpr/ppermute | solution.py:16
  167.0 4.3 %collective-permute-start.1 = (bf16[128,1,128]{2,0,1:T(8,128)(2,1)S(1)}, bf16[128,1,128]{2,0,1:T(8,128)(2,1)S(1)}, u32[]{:S(2)}, u32[]{:S(2)}) collective-permute-start(bf16[128,1,128]{2,0,1:T(8,128)(2,1)S(1)} %copy.76), channel_id=1, source_target_pairs={{4,0},{8,4},{12,8},{16,12},{20,16},{24,20},{28,24},{0,28},{5,1},{9... | collective-permute-start | bytes 98312 | tf_op jit(solution)/shard_map/while/body/eval_jaxpr/ppermute | solution.py:16
  171.4 9.7 %collective-permute-start.2 = (f32[128,1,128]{2,0,1:T(8,128)S(1)}, f32[128,1,128]{2,0,1:T(8,128)S(1)}, u32[]{:S(2)}, u32[]{:S(2)}) collective-permute-start(f32[128,1,128]{2,0,1:T(8,128)S(1)} %add.200), channel_id=1, source_target_pairs={{4,0},{8,4},{12,8},{16,12},{20,16},{24,20},{28,24},{0,28},{5,1},{9... | collective-permute-start | bytes 196616 | tf_op jit(solution)/shard_map/while/body/eval_jaxpr/ppermute | solution.py:16
  175.2 5.9 %collective-permute-start.3 = (f32[128,1,128]{2,0,1:T(8,128)S(1)}, f32[128,1,128]{2,0,1:T(8,128)S(1)}, u32[]{:S(2)}, u32[]{:S(2)}) collective-permute-start(f32[128,1,128]{2,0,1:T(8,128)S(1)} %add.201), channel_id=1, source_target_pairs={{4,0},{8,4},{12,8},{16,12},{20,16},{24,20},{28,24},{0,28},{5,1},{9... | collective-permute-start | bytes 196616 | tf_op jit(solution)/shard_map/while/body/eval_jaxpr/ppermute | solution.py:16
  175.3 4.6 %collective-permute-start = (bf16[128,1,128]{2,0,1:T(8,128)(2,1)S(1)}, bf16[128,1,128]{2,0,1:T(8,128)(2,1)S(1)}, u32[]{:S(2)}, u32[]{:S(2)}) collective-permute-start(bf16[128,1,128]{2,0,1:T(8,128)(2,1)S(1)} %copy.75), channel_id=1, source_target_pairs={{4,0},{8,4},{12,8},{16,12},{20,16},{24,20},{28,24},{0,28},{5,1},{9... | collective-permute-start | bytes 98312 | tf_op jit(solution)/shard_map/while/body/eval_jaxpr/ppermute | solution.py:16
  181.2 10.0 %collective-permute-start.2 = (f32[128,1,128]{2,0,1:T(8,128)S(1)}, f32[128,1,128]{2,0,1:T(8,128)S(1)}, u32[]{:S(2)}, u32[]{:S(2)}) collective-permute-start(f32[128,1,128]{2,0,1:T(8,128)S(1)} %add.200), channel_id=1, source_target_pairs={{4,0},{8,4},{12,8},{16,12},{20,16},{24,20},{28,24},{0,28},{5,1},{9... | collective-permute-start | bytes 196616 | tf_op jit(solution)/shard_map/while/body/eval_jaxpr/ppermute | solution.py:16
  185.4 5.7 %collective-permute-start.3 = (f32[128,1,128]{2,0,1:T(8,128)S(1)}, f32[128,1,128]{2,0,1:T(8,128)S(1)}, u32[]{:S(2)}, u32[]{:S(2)}) collective-permute-start(f32[128,1,128]{2,0,1:T(8,128)S(1)} %add.201), channel_id=1, source_target_pairs={{4,0},{8,4},{12,8},{16,12},{20,16},{24,20},{28,24},{0,28},{5,1},{9... | collective-permute-start | bytes 196616 | tf_op jit(solution)/shard_map/while/body/eval_jaxpr/ppermute | solution.py:16
  185.5 4.6 %collective-permute-start = (bf16[128,1,128]{2,0,1:T(8,128)(2,1)S(1)}, bf16[128,1,128]{2,0,1:T(8,128)(2,1)S(1)}, u32[]{:S(2)}, u32[]{:S(2)}) collective-permute-start(bf16[128,1,128]{2,0,1:T(8,128)(2,1)S(1)} %copy.75), channel_id=1, source_target_pairs={{4,0},{8,4},{12,8},{16,12},{20,16},{24,20},{28,24},{0,28},{5,1},{9... | collective-permute-start | bytes 98312 | tf_op jit(solution)/shard_map/while/body/eval_jaxpr/ppermute | solution.py:16
  187.0 4.2 %collective-permute-start.1 = (bf16[128,1,128]{2,0,1:T(8,128)(2,1)S(1)}, bf16[128,1,128]{2,0,1:T(8,128)(2,1)S(1)}, u32[]{:S(2)}, u32[]{:S(2)}) collective-permute-start(bf16[128,1,128]{2,0,1:T(8,128)(2,1)S(1)} %copy.76), channel_id=1, source_target_pairs={{4,0},{8,4},{12,8},{16,12},{20,16},{24,20},{28,24},{0,28},{5,1},{9... | collective-permute-start | bytes 98312 | tf_op jit(solution)/shard_map/while/body/eval_jaxpr/ppermute | solution.py:16
  191.3 9.4 %collective-permute-start.2 = (f32[128,1,128]{2,0,1:T(8,128)S(1)}, f32[128,1,128]{2,0,1:T(8,128)S(1)}, u32[]{:S(2)}, u32[]{:S(2)}) collective-permute-start(f32[128,1,128]{2,0,1:T(8,128)S(1)} %add.200), channel_id=1, source_target_pairs={{4,0},{8,4},{12,8},{16,12},{20,16},{24,20},{28,24},{0,28},{5,1},{9... | collective-permute-start | bytes 196616 | tf_op jit(solution)/shard_map/while/body/eval_jaxpr/ppermute | solution.py:16
  195.6 5.0 %collective-permute-start.3 = (f32[128,1,128]{2,0,1:T(8,128)S(1)}, f32[128,1,128]{2,0,1:T(8,128)S(1)}, u32[]{:S(2)}, u32[]{:S(2)}) collective-permute-start(f32[128,1,128]{2,0,1:T(8,128)S(1)} %add.201), channel_id=1, source_target_pairs={{4,0},{8,4},{12,8},{16,12},{20,16},{24,20},{28,24},{0,28},{5,1},{9... | collective-permute-start | bytes 196616 | tf_op jit(solution)/shard_map/while/body/eval_jaxpr/ppermute | solution.py:16
  195.7 4.6 %collective-permute-start = (bf16[128,1,128]{2,0,1:T(8,128)(2,1)S(1)}, bf16[128,1,128]{2,0,1:T(8,128)(2,1)S(1)}, u32[]{:S(2)}, u32[]{:S(2)}) collective-permute-start(bf16[128,1,128]{2,0,1:T(8,128)(2,1)S(1)} %copy.75), channel_id=1, source_target_pairs={{4,0},{8,4},{12,8},{16,12},{20,16},{24,20},{28,24},{0,28},{5,1},{9... | collective-permute-start | bytes 98312 | tf_op jit(solution)/shard_map/while/body/eval_jaxpr/ppermute | solution.py:16
  200.8 6.4 %collective-permute-start.4 = (f32[128,1,128]{0,2,1:T(8,128)S(1)}, f32[128,1,128]{0,2,1:T(8,128)S(1)}, u32[]{:S(2)}, u32[]{:S(2)}) collective-permute-start(f32[128,1,128]{0,2,1:T(8,128)S(1)} %add.165), channel_id=1, source_target_pairs={{4,0},{8,4},{12,8},{16,12},{20,16},{24,20},{28,24},{0,28},{5,1},{9... | collective-permute-start | bytes 196616 | tf_op jit(solution)/shard_map/ppermute | solution.py:16
  205.3 4.0 %collective-permute-start.5 = (bf16[128,1,128]{2,0,1:T(8,128)(2,1)S(1)}, bf16[128,1,128]{2,0,1:T(8,128)(2,1)S(1)}, u32[]{:S(2)}, u32[]{:S(2)}) collective-permute-start(bf16[128,1,128]{2,0,1:T(8,128)(2,1)S(1)} %add.167), channel_id=1, source_target_pairs={{4,0},{8,4},{12,8},{16,12},{20,16},{24,20},{28,24},{0,28},{5,1},{9... | collective-permute-start | bytes 98312 | tf_op jit(solution)/shard_map/ppermute | solution.py:16
  211.1 123.9 %reduce-scatter.5.cloned.1.call-start = ((), (), s32[]{:S(2)}) async-start(), calls=%async_computation.5 | async-start | bytes 4718592 | tf_op jit(solution)/shard_map/reduce_scatter | solution.py:201
  (5 other events, 69.1 us)
Sparse Core Ops, SparseCore 0:
  10.1 42.9 all-gather.3
  55.3 39.8 all-gather.5
  211.2 31.5 reduce-scatter.2
  246.3 88.6 reduce-scatter.4
where the time goes:
time: 345 us; the launch traced here: 344 us
  waiting for transfers between devices  207 us (60%)
  blocking collectives  57.6 us (17%)
  starting transfers between devices  41.5 us (12%)
  between operations  14 us (4%)
  matrix products  10.6 us (3%)
  local copies, waits for them, and re-layouts  8.03 us (2%)
  other arithmetic  4.45 us (1%)
    reduce_scatter x1, waiting for transfers between devices, body(): lax.psum_scatter(lax.dot_general(layer_input, both_grads, (((0,), (0,)),...  90.4 us
    all_gather x1, waiting for transfers between devices, body(): lax.all_gather(w_key, 'seq', axis=0, tiled=True)  42 us
    ppermute x30, starting transfers between devices, passed_along(): return lax.ppermute(block, axis, route)  41.3 us
    ppermute x30, waiting for transfers between devices, passed_along(): return lax.ppermute(block, axis, route)  33.4 us
    all_gather x1, blocking collectives, body(): lax.all_gather(values, 'seq', axis=0, tiled=True)  30.8 us
    reduce_scatter x1, waiting for transfers between devices, body(): lax.psum_scatter(partial_input, 'fsdp', scatter_dimension=1, tiled=True)  27 us
    all_gather x1, blocking collectives, body(): lax.all_gather(keys, 'seq', axis=0, tiled=True)  26.8 us
    all_gather x1, waiting for transfers between devices, body(): lax.all_gather(w_value, 'seq', axis=0, tiled=True)  13.2 us
  transfers between devices with their start and end apart: 34, of which 20 were waited for; matrix products, arithmetic and copies ran while one was open for 3% of the time, Pallas kernels for 0%

commit v1 on v0

v1 whole, which is shorter than its diff:
```python
import functools

import jax
import jax.numpy as jnp
import numpy as np
from jax import lax
from jax.experimental import pallas as pl
from jax.experimental.pallas import tpu as pltpu
from jax.sharding import PartitionSpec as P

HD = 128
ROPE_BASE = 500000.0
NEG = -1e30
MESH = pl.DeviceIdType.MESH
F32 = jnp.float32
BF16 = jnp.bfloat16


def loop(low, high, step):
    def run(i, carry):
        step(i)
        return carry

    lax.fori_loop(low, high, run, 0)


def dot_nn(a, b):
    return lax.dot_general(a, b, (((1,), (0,)), ((), ())), preferred_element_type=F32)


def dot_nt(a, b):
    return lax.dot_general(a, b, (((1,), (1,)), ((), ())), preferred_element_type=F32)


def dot_tn(a, b):
    return lax.dot_general(a, b, (((0,), (0,)), ((), ())), preferred_element_type=F32)


def kernel(cfg, *refs):
    n, nf, exchange = cfg
    q_ref, x_ref, wk_ref, wv_ref, g_ref, freq_ref = refs[:6]
    refs = refs[6:]
    if not exchange:
        xt_in = refs[0]
        refs = refs[1:]
    ao_ref, gq_ref, gi_ref, gwk_ref, gwv_ref = refs[:5]
    (wk_all, wv_all, kv_all, dkv_all, xt, q_st, g_st, o_acc, dq_acc, m_acc, l_acc, s_scr,
     rs_send, rs_recv, own_dkv, cos_scr, sin_scr, gi_send, gi_recv, gi_own,
     wk_s, wk_r, wv_s, wv_r, kv_s, kv_r, dkv_s, dkv_r, x_s, x_r, xf_s, xf_r,
     rs_s, rs_r, gi_s, gi_r) = refs[5:]
    tok = x_ref.shape[0]
    rows, cols = wk_ref.shape
    heads = cols // HD
    group = q_ref.shape[1] // cols
    m_rows = group * tok
    part = rows // nf
    width = gi_ref.shape[1]
    scale = HD ** (-0.5)
    s = lax.axis_index("seq")
    f = lax.axis_index("fsdp")
    inner = 2 if n % 2 == 0 else 1
    outer = n // inner
    z = s // inner
    y = s % inner
    mate = z * inner + (inner - 1 - y)

    def copy(src, dst, send, recv, dev):
        return pltpu.make_async_remote_copy(
            src_ref=src, dst_ref=dst, send_sem=send, recv_sem=recv, device_id=dev,
            device_id_type=MESH,
        )

    barrier = pltpu.get_barrier_semaphore()

    def greet_seq(d):
        pl.semaphore_signal(
            barrier, inc=1, device_id=((s + d) % n, f), device_id_type=MESH)

    def greet_fsdp(d):
        pl.semaphore_signal(
            barrier, inc=1, device_id=(s, (f + d) % nf), device_id_type=MESH)

    loop(1, n, greet_seq)
    loop(1, nf, greet_fsdp)
    pl.semaphore_wait(barrier, n + nf - 2)

    class Gather:
        def __init__(self, own, slot, send, recv):
            self.own, self.slot, self.send, self.recv = own, slot, send, recv

        def outgoing(self, d):
            return copy(self.own, self.slot(s), self.send.at[d], self.recv.at[s],
                        ((z + d) % outer * inner + y, f))

        def to_mate(self):
            return copy(self.own, self.slot(s), self.send.at[0], self.recv.at[s], (mate, f))

        def arrived(self, b):
            copy(self.own, self.slot(b), self.send.at[0], self.recv.at[b], (mate, f)).wait_recv()

        def pass_on(self, d):
            b = (z - d + outer) % outer * inner + y
            return copy(self.slot(b), self.slot(b), self.send.at[outer + d], self.recv.at[b],
                        (mate, f))

        def start(self):
            if inner == 2:
                self.to_mate().start()
            loop(1, outer, lambda d: self.outgoing(d).start())

        def forward(self):
            def step(d):
                self.arrived((z - d + outer) % outer * inner + y)
                if inner == 2:
                    self.pass_on(d).start()

            loop(1, outer, step)

        def finish(self):
            if inner == 2:
                loop(0, outer, lambda d: self.arrived(
                    (z - d + outer) % outer * inner + (inner - 1 - y)))

        def drain(self):
            if inner == 2:
                self.to_mate().wait_send()
            loop(1, outer, lambda d: self.outgoing(d).wait_send())
            if inner == 2:
                loop(1, outer, lambda d: self.pass_on(d).wait_send())

    def row_slot(ref, size):
        return lambda b: ref.at[pl.ds(pl.multiple_of(b * size, size), size)]

    wk_gather = Gather(wk_ref, row_slot(wk_all, rows), wk_s, wk_r)
    wv_gather = Gather(wv_ref, row_slot(wv_all, rows), wv_s, wv_r)
    kv_slot = row_slot(kv_all, tok)
    kv_gather = Gather(kv_slot(s), kv_slot, kv_s, kv_r)
    dkv_slot = row_slot(dkv_all, tok)
    dkv_gather = Gather(dkv_slot(s), dkv_slot, dkv_s, dkv_r)

    wk_gather.start()
    wv_gather.start()

    if exchange:
        def x_src(b):
            return x_ref.at[:, pl.ds(pl.multiple_of(b * rows + f * part, part), part)]

        def x_copy(d):
            b = (s + d) % n
            return copy(x_src(b), xt.at[f, pl.ds(pl.multiple_of(s * tok, tok), tok)],
                        x_s.at[d], x_r.at[s], (b, f))

        def x_arrived(d):
            b = (s + d) % n
            copy(x_src(b), xt.at[f, pl.ds(pl.multiple_of(b * tok, tok), tok)],
                 x_s.at[d], x_r.at[b], (b, f)).wait_recv()

        def xf_copy(d):
            return copy(xt.at[f], xt.at[f], xf_s.at[d], xf_r.at[f], (s, (f + d) % nf))

        def xf_arrived(d):
            b = (f + d) % nf
            copy(xt.at[f], xt.at[b], xf_s.at[d], xf_r.at[b], (s, b)).wait_recv()

        loop(1, n, lambda d: x_copy(d).start())
        xt[f, pl.ds(pl.multiple_of(s * tok, tok), tok), :] = x_ref[
            :, pl.ds(pl.multiple_of(s * rows + f * part, part), part)]

    wk_all[pl.ds(pl.multiple_of(s * rows, rows), rows), :] = wk_ref[...]
    wv_all[pl.ds(pl.multiple_of(s * rows, rows), rows), :] = wv_ref[...]
    for h in range(heads):
        for g in range(group):
            c = (h * group + g) * HD
            q_st[h, g * tok:(g + 1) * tok, :] = q_ref[:, c:c + HD]
            g_st[h, g * tok:(g + 1) * tok, :] = g_ref[:, c:c + HD]
    lane = lax.broadcasted_iota(jnp.int32, (tok, HD), 1)
    position = (s * tok + lax.broadcasted_iota(jnp.int32, (tok, HD), 0)).astype(F32)
    angle = position * freq_ref[...]
    cos_scr[...] = jnp.cos(angle)
    sin_scr[...] = jnp.where(lane < HD // 2, -jnp.sin(angle), jnp.sin(angle))

    wk_gather.forward()
    wv_gather.forward()
    wk_gather.finish()
    wv_gather.finish()

    key_lin = dot_nn(x_ref[...], wk_all[...])
    value_lin = dot_nn(x_ref[...], wv_all[...])
    own_rows = pl.ds(pl.multiple_of(s * tok, tok), tok)
    for h in range(heads):
        lin = key_lin[:, h * HD:(h + 1) * HD]
        turned = lin * cos_scr[...] + pltpu.roll(lin, HD // 2, 1) * sin_scr[...]
        kv_all[own_rows, h * HD:(h + 1) * HD] = turned.astype(BF16)
    kv_all[own_rows, cols:] = value_lin.astype(BF16)
    kv_gather.start()

    if exchange:
        loop(1, n, x_arrived)
        loop(1, nf, lambda d: xf_copy(d).start())

    kv_gather.forward()
    kv_gather.finish()

    def key_of(j, h):
        return kv_all[pl.ds(pl.multiple_of(j * tok, tok), tok), h * HD:(h + 1) * HD]

    def value_of(j, h):
        return kv_all[pl.ds(pl.multiple_of(j * tok, tok), tok), cols + h * HD:cols + (h + 1) * HD]

    deltas, inverses = [], []
    for h in range(heads):
        m_acc[...] = jnp.full(m_acc.shape, NEG, F32)
        l_acc[...] = jnp.zeros(l_acc.shape, F32)
        o_acc[...] = jnp.zeros(o_acc.shape, F32)

        def score(j):
            sc = dot_nt(q_st[h], key_of(j, h)) * scale
            row = lax.broadcasted_iota(jnp.int32, (m_rows, tok), 0) % tok
            col = lax.broadcasted_iota(jnp.int32, (m_rows, tok), 1)
            sc = jnp.where(col + j * tok <= row + s * tok, sc, NEG)
            s_scr[h * n + j] = sc
            m_acc[...] = jnp.maximum(m_acc[...], sc)

        loop(0, s + 1, score)
        top = jnp.max(m_acc[...], axis=1, keepdims=True)

        def weigh(j):
            e = jnp.exp(s_scr[h * n + j] - top)
            s_scr[h * n + j] = e
            l_acc[...] += e
            o_acc[...] += dot_nn(e.astype(BF16), value_of(j, h))

        loop(0, s + 1, weigh)
        inverse = 1.0 / jnp.sum(l_acc[...], axis=1, keepdims=True)
        out = o_acc[...] * inverse
        delta = jnp.sum(g_st[h].astype(F32) * out, axis=1, keepdims=True)
        for g in range(group):
            c = (h * group + g) * HD
            ao_ref[:, c:c + HD] = out[g * tok:(g + 1) * tok].astype(BF16)
        deltas.append(delta)
        inverses.append(inverse)

    dq_acc[...] = jnp.zeros(dq_acc.shape, F32)

    def backward(j, h):
        p = s_scr[h * n + j] * inverses[h]
        dp = dot_nt(g_st[h], value_of(j, h))
        ds = (p * (dp - deltas[h])).astype(BF16)
        dv = dot_tn(p.astype(BF16), g_st[h])
        dk = dot_tn(ds, q_st[h])
        dq_acc[h] += dot_nn(ds, key_of(j, h))
        return dk, dv

    def rs_copy(j):
        return copy(rs_send.at[j], rs_recv.at[s], rs_s.at[j], rs_r.at[s], (j, f))

    def give(j):
        for h in range(heads):
            dk, dv = backward(j, h)
            rs_send[j, :, h * HD:(h + 1) * HD] = dk.astype(BF16)
            rs_send[j, :, cols + h * HD:cols + (h + 1) * HD] = dv.astype(BF16)
        rs_copy(j).start()

    loop(0, s, give)
    for h in range(heads):
        dk, dv = backward(s, h)
        own_dkv[:, h * HD:(h + 1) * HD] = dk
        own_dkv[:, cols + h * HD:cols + (h + 1) * HD] = dv
        for g in range(group):
            c = (h * group + g) * HD
            gq_ref[:, c:c + HD] = (dq_acc[h, g * tok:(g + 1) * tok] * scale).astype(BF16)

    def take(j):
        copy(rs_send.at[0], rs_recv.at[j], rs_s.at[0], rs_r.at[j], (mate, f)).wait_recv()
        own_dkv[...] += rs_recv[j].astype(F32)

    loop(s + 1, n, take)
    for h in range(heads):
        lin = own_dkv[:, h * HD:(h + 1) * HD] * scale
        turned = lin * cos_scr[...] - pltpu.roll(lin, HD // 2, 1) * sin_scr[...]
        dkv_all[own_rows, h * HD:(h + 1) * HD] = turned.astype(BF16)
    dkv_all[own_rows, cols:] = own_dkv[:, cols:].astype(BF16)
    dkv_gather.start()

    def input_term(b):
        at = pl.ds(pl.multiple_of(b * width, width), width)
        return (dot_nt(dkv_all[own_rows, :cols], wk_all[at, :])
                + dot_nt(dkv_all[own_rows, cols:], wv_all[at, :]))

    def gi_copy(d):
        return copy(gi_send.at[d], gi_recv.at[f], gi_s.at[d], gi_r.at[f], (s, (f + d) % nf))

    def gi_give(d):
        gi_send[d] = input_term((f + d) % nf).astype(BF16)
        gi_copy(d).start()

    loop(1, nf, gi_give)
    gi_own[...] = input_term(f)
    if exchange:
        loop(1, nf, xf_arrived)
    dkv_gather.forward()
    dkv_gather.finish()

    total_tok = n * tok
    step = min(total_tok, 1024)
    for i in range(nf if exchange else 1):
        grad = None
        for at in range(0, total_tok, step):
            left = xt[i, at:at + step, :] if exchange else xt_in[at:at + step, :]
            term = dot_tn(left, dkv_all[at:at + step, :])
            grad = term if grad is None else grad + term
        count = grad.shape[0]
        gwk_ref[i * count:(i + 1) * count, :] = grad[:, :cols]
        gwv_ref[i * count:(i + 1) * count, :] = grad[:, cols:]

    def gi_take(d):
        b = (f + d) % nf
        copy(gi_send.at[d], gi_recv.at[b], gi_s.at[d], gi_r.at[b], (s, b)).wait_recv()
        gi_own[...] += gi_recv[b].astype(F32)

    loop(1, nf, gi_take)
    gi_ref[...] = gi_own[...].astype(BF16)

    for gather in (wk_gather, wv_gather, kv_gather, dkv_gather):
        gather.drain()
    if exchange:
        loop(1, n, lambda d: x_copy(d).wait_send())
        loop(1, nf, lambda d: xf_copy(d).wait_send())
    loop(0, s, lambda j: rs_copy(j).wait_send())
    loop(1, nf, lambda d: gi_copy(d).wait_send())


def body(n, nf, queries, layer_input, w_key, w_value, grad_out):
    tok, depth = layer_input.shape
    rows, cols = w_key.shape
    heads = cols // HD
    group = queries.shape[1] // cols
    m_rows = group * tok
    part = rows // nf
    exchange = part % 128 == 0
    half = HD // 2
    freq = np.float32(ROPE_BASE) ** (-(np.arange(half, dtype=np.float32) * np.float32(2.0 / HD)))
    freq = jnp.asarray(np.concatenate([freq, freq])[None, :], F32)
    operands = [queries, layer_input, w_key, w_value, grad_out, freq]
    if not exchange:
        operands.append(
            lax.all_to_all(layer_input, "seq", split_axis=1, concat_axis=0, tiled=True))
    width = depth // nf
    x_rows = n * tok if exchange else 16
    x_cols = part if exchange else 128
    vmem = pltpu.VMEM
    dma = pltpu.SemaphoreType.DMA
    scratch = [
        vmem((depth, cols), BF16), vmem((depth, cols), BF16),
        vmem((n * tok, 2 * cols), BF16), vmem((n * tok, 2 * cols), BF16),
        vmem((nf, x_rows, x_cols), BF16),
        vmem((heads, m_rows, HD), BF16), vmem((heads, m_rows, HD), BF16),
        vmem((m_rows, HD), F32), vmem((heads, m_rows, HD), F32),
        vmem((m_rows, tok), F32), vmem((m_rows, tok), F32),
        vmem((heads * n, m_rows, tok), F32),
        vmem((n, tok, 2 * cols), BF16), vmem((n, tok, 2 * cols), BF16),
        vmem((tok, 2 * cols), F32),
        vmem((tok, HD), F32), vmem((tok, HD), F32),
        vmem((nf, tok, width), BF16), vmem((nf, tok, width), BF16), vmem((tok, width), F32),
    ]
    for _ in range(4):
        scratch += [dma((2 * n,)), dma((n,))]
    scratch += [dma((n,)), dma((n,)), dma((nf,)), dma((nf,))]
    scratch += [dma((n,)), dma((n,)), dma((nf,)), dma((nf,))]
    out_shape = [
        jax.ShapeDtypeStruct(queries.shape, BF16),
        jax.ShapeDtypeStruct(queries.shape, BF16),
        jax.ShapeDtypeStruct((tok, width), BF16),
        jax.ShapeDtypeStruct((rows, cols), F32),
        jax.ShapeDtypeStruct((rows, cols), F32),
    ]
    spec = pl.BlockSpec(memory_space=pltpu.VMEM)
    return tuple(pl.pallas_call(
        functools.partial(kernel, (n, nf, exchange)),
        out_shape=out_shape,
        in_specs=[spec] * len(operands),
        out_specs=[spec] * len(out_shape),
        scratch_shapes=scratch,
        compiler_params=pltpu.CompilerParams(
            collective_id=0, has_side_effects=True, vmem_limit_bytes=60 * 1024 * 1024),
    )(*operands))


def solution(mesh):
    placed = (
        P("seq", "fsdp"),
        P("seq", None),
        P("seq", "fsdp"),
        P("seq", "fsdp"),
        P("seq", "fsdp"),
    )
    return jax.shard_map(
        functools.partial(body, mesh.shape["seq"], mesh.shape["fsdp"]),
        mesh=mesh,
        in_specs=placed,
        out_specs=(P("seq", "fsdp"),) * 5,
        check_vma=False,
    )
```

time: 345 us -> 86.9 us (0.25)
  waiting for transfers between devices: 207 us -> 0 us
  Pallas kernels: 0 us -> 80.1 us
  blocking collectives: 57.6 us -> 0 us
  starting transfers between devices: 41.5 us -> 0 us
  between operations: 14 us -> 0.66 us
  matrix products: 10.6 us -> 0 us
  other arithmetic: 4.45 us -> 0 us
    reduce_scatter x2 -> x0, waiting for transfers between devices: 117 us -> none  [the longest x1 90.4 us: body(): lax.psum_scatter(lax.dot_general(layer_input, both_grads, (((0,), (0,)),...]
    pallas_call x0 -> x1, Pallas kernels: none -> 80.1 us  [body(): pl.pallas_call(functools.partial(kernel, (n, nf, exchange)), out_shape=ou...]
    all_gather x2 -> x0, blocking collectives: 57.6 us -> none  [the longest x1 30.8 us: body(): lax.all_gather(values, 'seq', axis=0, tiled=True)]
    all_gather x2 -> x0, waiting for transfers between devices: 55.2 us -> none  [the longest x1 42 us: body(): lax.all_gather(w_key, 'seq', axis=0, tiled=True)]
    ppermute x30 -> x0, starting transfers between devices: 41.3 us -> none  [passed_along(): return lax.ppermute(block, axis, route)]
    ppermute x30 -> x0, waiting for transfers between devices: 33.4 us -> none  [passed_along(): return lax.ppermute(block, axis, route)]
    dot_general x12 -> x0, matrix products: 10.6 us -> none  [the longest x1 2.76 us: body(): lax.dot_general(layer_input, both_grads, (((0,), (0,)), ((), ())), prefer...]
  transfers between devices with their start and end apart: 34 -> 0, of which waited for: 20 -> 0; matrix products, arithmetic and copies ran while one was open for 3% -> 0% of each run, Pallas kernels for 0% -> 0%
where the time goes in v1:
time: 86.9 us; the launch traced here: 85.8 us
  Pallas kernels  80.1 us (92%)
  local copies, waits for them, and re-layouts  5.07 us (6%)
    pallas_call x1, Pallas kernels, body(): pl.pallas_call(functools.partial(kernel, (n, nf, exchange)), out_shape=ou...  80.1 us
    unnamed x13, local copies, waits for them, and re-layouts  5.07 us

profile of v1, /device:TPU:0, one launch (start us, length us, event | category | flops | bytes accessed | tf_op | source)
XLA Modules:
  0.0 85.8 jit_solution(10912805513715453013)
XLA Ops:
  0.6 80.1 %shard_map.101 = (bf16[128,512]{1,0:T(8,128)(2,1)}, bf16[128,512]{1,0:T(8,128)(2,1)}, bf16[128,1024]{1,0:T(8,128)(2,1)}, f32[512,128]{1,0:T(8,128)}, f32[512,128]{1,0:T(8,128)}) custom-call(bf16[128,512]{1,0:T(8,128)(2,1)} %refs_0_.1, bf16[128,4096]{1,0:T(8,128)(2,1)} %refs_1_.1, bf16[512,128]{1,0:T(8,128)(2,1)} %refs_2_.1, bf16[512,128]{1,0:T(8,128)(2,1)} %refs_3_.1, ...), custom_call_target="tpu_custom_call" | custom-call | tf_op jit(solution)/shard_map/pallas_call | solution.py:378
  80.7 0.0 copy-start.3
  80.8 0.0 copy-start.2
  80.8 1.6 %copy.16 = bf16[128,512]{1,0:T(8,128)(2,1)} copy(bf16[128,512]{1,0:T(8,128)(2,1)} %get-tuple-element.10) | data formatting | bytes 262144
  82.4 0.0 copy-done.3
  82.4 0.7 copy.17
  83.0 0.0 copy-done.2
  83.0 0.0 copy-start.1
  83.0 0.7 copy.18
  83.8 0.3 copy-done.1
  84.1 0.0 copy-start
  84.1 0.7 copy.19
  84.8 0.3 copy-done
  85.1 0.7 copy.20
Async XLA Ops:
  80.7 1.6 %copy-start.3 = (bf16[128,512]{1,0:T(8,128)(2,1)S(1)}, bf16[128,512]{1,0:T(8,128)(2,1)}, u32[]{:S(2)}) copy-start(bf16[128,512]{1,0:T(8,128)(2,1)} %get-tuple-element.11) | copy-start | bytes 393220
  80.8 2.3 %copy-start.2 = (bf16[128,1024]{1,0:T(8,128)(2,1)S(1)}, bf16[128,1024]{1,0:T(8,128)(2,1)}, u32[]{:S(2)}) copy-start(bf16[128,1024]{1,0:T(8,128)(2,1)} %get-tuple-element.12) | copy-start | bytes 786436
  83.0 1.0 %copy-start.1 = (f32[512,128]{1,0:T(8,128)S(1)}, f32[512,128]{1,0:T(8,128)}, u32[]{:S(2)}) copy-start(f32[512,128]{1,0:T(8,128)} %get-tuple-element.13) | copy-start | bytes 786436
  84.1 1.0 %copy-start = (f32[512,128]{1,0:T(8,128)S(1)}, f32[512,128]{1,0:T(8,128)}, u32[]{:S(2)}) copy-start(f32[512,128]{1,0:T(8,128)} %get-tuple-element.14) | copy-start | bytes 786436

commit v2 on v1

--- a/solution.py
+++ b/solution.py
@@ -38,7 +38,7 @@
 
 def kernel(cfg, *refs):
     n, nf, exchange = cfg
-    q_ref, x_ref, wk_ref, wv_ref, g_ref, freq_ref = refs[:6]
+    q_hbm, x_hbm, wk_ref, wv_ref, g_hbm, freq_ref = refs[:6]
     refs = refs[6:]
     if not exchange:
         xt_in = refs[0]
@@ -47,7 +47,7 @@
     (wk_all, wv_all, kv_all, dkv_all, xt, q_st, g_st, o_acc, dq_acc, m_acc, l_acc, s_scr,
      rs_send, rs_recv, own_dkv, cos_scr, sin_scr, gi_send, gi_recv, gi_own,
      wk_s, wk_r, wv_s, wv_r, kv_s, kv_r, dkv_s, dkv_r, x_s, x_r, xf_s, xf_r,
-     rs_s, rs_r, gi_s, gi_r) = refs[5:]
+     rs_s, rs_r, gi_s, gi_r, q_ref, x_ref, g_ref, in_s) = refs[5:]
     tok = x_ref.shape[0]
     rows, cols = wk_ref.shape
     heads = cols // HD
@@ -82,6 +82,15 @@
 
     loop(1, n, greet_seq)
     loop(1, nf, greet_fsdp)
+    mine = pl.ds(pl.multiple_of(s * rows, rows), rows)
+    loads = [
+        pltpu.make_async_copy(src, dst, in_s.at[i])
+        for i, (src, dst) in enumerate((
+            (wk_ref, wk_all.at[mine]), (wv_ref, wv_all.at[mine]),
+            (x_hbm, x_ref), (q_hbm, q_ref), (g_hbm, g_ref)))
+    ]
+    for load in loads:
+        load.start()
     pl.semaphore_wait(barrier, n + nf - 2)
 
     class Gather:
@@ -128,18 +137,75 @@
             if inner == 2:
                 loop(1, outer, lambda d: self.pass_on(d).wait_send())
 
+    class Line(Gather):
+        def hop(self, b, way):
+            ref = self.slot(b)
+            dev = (z + 1) * inner + y if way == 0 else (z - 1) * inner + y if way == 1 else mate
+            return copy(ref, ref, self.send.at[way * n + b], self.recv.at[b], (dev, f))
+
+        def first(self, way):
+            dev = (z + 1) * inner + y if way == 0 else (z - 1) * inner + y if way == 1 else mate
+            return copy(self.own, self.slot(s), self.send.at[way * n + s], self.recv.at[s],
+                        (dev, f))
+
+        def start(self):
+            pl.when(z < outer - 1)(lambda: self.first(0).start())
+            pl.when(z > 0)(lambda: self.first(1).start())
+            if inner == 2:
+                self.first(2).start()
+
+        def relay(self, d, act):
+            below = (z - d) * inner + y
+            above = (z + d) * inner + y
+
+            @pl.when(z >= d)
+            def _():
+                if act == "start":
+                    self.arrived(below)
+                for way in (0, 2) if inner == 2 else (0,):
+                    def go(way=way):
+                        getattr(self.hop(below, way), act)()
+                    if way == 0:
+                        pl.when(z < outer - 1)(go)
+                    else:
+                        go()
+
+            @pl.when(z + d < outer)
+            def _():
+                if act == "start":
+                    self.arrived(above)
+                for way in (1, 2) if inner == 2 else (1,):
+                    def go(way=way):
+                        getattr(self.hop(above, way), act)()
+                    if way == 1:
+                        pl.when(z > 0)(go)
+                    else:
+                        go()
+
+        def drain(self):
+            pl.when(z < outer - 1)(lambda: self.first(0).wait_send())
+            pl.when(z > 0)(lambda: self.first(1).wait_send())
+            if inner == 2:
+                self.first(2).wait_send()
+            loop(1, outer, lambda d: self.relay(d, "wait_send"))
+
     def row_slot(ref, size):
         return lambda b: ref.at[pl.ds(pl.multiple_of(b * size, size), size)]
 
-    wk_gather = Gather(wk_ref, row_slot(wk_all, rows), wk_s, wk_r)
-    wv_gather = Gather(wv_ref, row_slot(wv_all, rows), wv_s, wv_r)
+    wk_slot, wv_slot = row_slot(wk_all, rows), row_slot(wv_all, rows)
+    wk_gather = Line(wk_slot(s), wk_slot, wk_s, wk_r)
+    wv_gather = Line(wv_slot(s), wv_slot, wv_s, wv_r)
     kv_slot = row_slot(kv_all, tok)
     kv_gather = Gather(kv_slot(s), kv_slot, kv_s, kv_r)
     dkv_slot = row_slot(dkv_all, tok)
     dkv_gather = Gather(dkv_slot(s), dkv_slot, dkv_s, dkv_r)
 
+    loads[0].wait()
     wk_gather.start()
+    loads[1].wait()
     wv_gather.start()
+    for load in loads[2:]:
+        load.wait()
 
     if exchange:
         def x_src(b):
@@ -162,12 +228,9 @@
             b = (f + d) % nf
             copy(xt.at[f], xt.at[b], xf_s.at[d], xf_r.at[b], (s, b)).wait_recv()
 
-        loop(1, n, lambda d: x_copy(d).start())
         xt[f, pl.ds(pl.multiple_of(s * tok, tok), tok), :] = x_ref[
             :, pl.ds(pl.multiple_of(s * rows + f * part, part), part)]
 
-    wk_all[pl.ds(pl.multiple_of(s * rows, rows), rows), :] = wk_ref[...]
-    wv_all[pl.ds(pl.multiple_of(s * rows, rows), rows), :] = wv_ref[...]
     for h in range(heads):
         for g in range(group):
             c = (h * group + g) * HD
@@ -179,8 +242,11 @@
     cos_scr[...] = jnp.cos(angle)
     sin_scr[...] = jnp.where(lane < HD // 2, -jnp.sin(angle), jnp.sin(angle))
 
-    wk_gather.forward()
-    wv_gather.forward()
+    def relay_weights(d):
+        wk_gather.relay(d, "start")
+        wv_gather.relay(d, "start")
+
+    loop(1, outer, relay_weights)
     wk_gather.finish()
     wv_gather.finish()
 
@@ -195,8 +261,7 @@
     kv_gather.start()
 
     if exchange:
-        loop(1, n, x_arrived)
-        loop(1, nf, lambda d: xf_copy(d).start())
+        loop(1, n, lambda d: x_copy(d).start())
 
     kv_gather.forward()
     kv_gather.finish()
@@ -240,6 +305,10 @@
         deltas.append(delta)
         inverses.append(inverse)
 
+    if exchange:
+        loop(1, n, x_arrived)
+        loop(1, nf, lambda d: xf_copy(d).start())
+
     dq_acc[...] = jnp.zeros(dq_acc.shape, F32)
 
     def backward(j, h):
@@ -287,15 +356,45 @@
         return (dot_nt(dkv_all[own_rows, :cols], wk_all[at, :])
                 + dot_nt(dkv_all[own_rows, cols:], wv_all[at, :]))
 
-    def gi_copy(d):
-        return copy(gi_send.at[d], gi_recv.at[f], gi_s.at[d], gi_r.at[f], (s, (f + d) % nf))
-
-    def gi_give(d):
-        gi_send[d] = input_term((f + d) % nf).astype(BF16)
-        gi_copy(d).start()
-
-    loop(1, nf, gi_give)
-    gi_own[...] = input_term(f)
+    cores = 2 if nf % 2 == 0 else 1
+    chips = nf // cores
+    chip = f // cores
+    core = f % cores
+    twin = chip * cores + (cores - 1 - core)
+
+    def gi_twin(o):
+        return copy(gi_send.at[o], gi_recv.at[o], gi_s.at[o], gi_r.at[o], (s, twin))
+
+    def gi_far(d):
+        return copy(gi_send.at[chips + d], gi_recv.at[chips + chip], gi_s.at[chips + d],
+                    gi_r.at[chips + chip], (s, (chip + d) % chips * cores + core))
+
+    def twin_term(d):
+        o = (chip + d) % chips
+        gi_send[o] = input_term(o * cores + 1 - core).astype(BF16)
+        gi_twin(o).start()
+
+    def own_term(d):
+        o = (chip + d) % chips
+        gi_own[o] = input_term(o * cores + core)
+
+    def join(d):
+        o = (chip + d) % chips
+        gi_twin(o).wait_recv()
+        gi_own[o] += gi_recv[o].astype(F32)
+
+    def far_term(d):
+        if cores == 2:
+            join(d)
+        gi_send[chips + d] = gi_own[(chip + d) % chips].astype(BF16)
+        gi_far(d).start()
+
+    if cores == 2:
+        loop(1, chips + 1, twin_term)
+    loop(1, chips + 1, own_term)
+    loop(1, chips, far_term)
+    if cores == 2:
+        join(0)
     if exchange:
         loop(1, nf, xf_arrived)
     dkv_gather.forward()
@@ -314,12 +413,13 @@
         gwv_ref[i * count:(i + 1) * count, :] = grad[:, cols:]
 
     def gi_take(d):
-        b = (f + d) % nf
-        copy(gi_send.at[d], gi_recv.at[b], gi_s.at[d], gi_r.at[b], (s, b)).wait_recv()
-        gi_own[...] += gi_recv[b].astype(F32)
-
-    loop(1, nf, gi_take)
-    gi_ref[...] = gi_own[...].astype(BF16)
+        b = (chip + d) % chips
+        copy(gi_send.at[chips + d], gi_recv.at[chips + b], gi_s.at[chips + d],
+             gi_r.at[chips + b], (s, b * cores + core)).wait_recv()
+        gi_own[chip] += gi_recv[chips + b].astype(F32)
+
+    loop(1, chips, gi_take)
+    gi_ref[...] = gi_own[chip].astype(BF16)
 
     for gather in (wk_gather, wv_gather, kv_gather, dkv_gather):
         gather.drain()
@@ -327,7 +427,19 @@
         loop(1, n, lambda d: x_copy(d).wait_send())
         loop(1, nf, lambda d: xf_copy(d).wait_send())
     loop(0, s, lambda j: rs_copy(j).wait_send())
-    loop(1, nf, lambda d: gi_copy(d).wait_send())
+    if cores == 2:
+        loop(0, chips, lambda o: gi_twin(o).wait_send())
+    loop(1, chips, lambda d: gi_far(d).wait_send())
+
+
+def publish(*refs):
+    count = len(refs) // 2
+    sems = refs[-1]
+    moves = [pltpu.make_async_copy(refs[i], refs[count + i], sems.at[i]) for i in range(count)]
+    for move in moves:
+        move.start()
+    for move in moves:
+        move.wait()
 
 
 def body(n, nf, queries, layer_input, w_key, w_value, grad_out):
@@ -361,12 +473,15 @@
         vmem((n, tok, 2 * cols), BF16), vmem((n, tok, 2 * cols), BF16),
         vmem((tok, 2 * cols), F32),
         vmem((tok, HD), F32), vmem((tok, HD), F32),
-        vmem((nf, tok, width), BF16), vmem((nf, tok, width), BF16), vmem((tok, width), F32),
+        vmem((2 * nf, tok, width), BF16), vmem((2 * nf, tok, width), BF16),
+        vmem((nf, tok, width), F32),
     ]
     for _ in range(4):
-        scratch += [dma((2 * n,)), dma((n,))]
+        scratch += [dma((3 * n,)), dma((n,))]
     scratch += [dma((n,)), dma((n,)), dma((nf,)), dma((nf,))]
-    scratch += [dma((n,)), dma((n,)), dma((nf,)), dma((nf,))]
+    scratch += [dma((n,)), dma((n,)), dma((2 * nf,)), dma((2 * nf,))]
+    scratch += [vmem(queries.shape, BF16), vmem((tok, depth), BF16), vmem(queries.shape, BF16),
+                dma((5,))]
     out_shape = [
         jax.ShapeDtypeStruct(queries.shape, BF16),
         jax.ShapeDtypeStruct(queries.shape, BF16),
@@ -375,15 +490,24 @@
         jax.ShapeDtypeStruct((rows, cols), F32),
     ]
     spec = pl.BlockSpec(memory_space=pltpu.VMEM)
-    return tuple(pl.pallas_call(
+    whole = pl.BlockSpec(memory_space=pl.ANY)
+    results = pl.pallas_call(
         functools.partial(kernel, (n, nf, exchange)),
-        out_shape=out_shape,
-        in_specs=[spec] * len(operands),
+        out_shape=[pltpu.VMEM(o.shape, o.dtype) for o in out_shape],
+        in_specs=[whole] * 5 + [spec] * (len(operands) - 5),
         out_specs=[spec] * len(out_shape),
         scratch_shapes=scratch,
         compiler_params=pltpu.CompilerParams(
             collective_id=0, has_side_effects=True, vmem_limit_bytes=60 * 1024 * 1024),
-    )(*operands))
+    )(*operands)
+    return tuple(pl.pallas_call(
+        publish,
+        out_shape=out_shape,
+        in_specs=[spec] * len(out_shape),
+        out_specs=[whole] * len(out_shape),
+        scratch_shapes=[dma((len(out_shape),))],
+        compiler_params=pltpu.CompilerParams(vmem_limit_bytes=8 * 1024 * 1024),
+    )(*results))
 
 
 def solution(mesh):

time: 86.9 us -> 69.9 us (0.80); the launches traced: 85.8 us -> 69.8 us
  Pallas kernels: 80.1 us -> 69.1 us
  local copies, waits for them, and re-layouts: 5.07 us -> 0 us
    pallas_call x1 -> x2, Pallas kernels: 80.1 us -> 69.1 us  [the longest x1 68.1 us: body(): pl.pallas_call(functools.partial(kernel, (n, nf, exchange)), out_shape=[p...]
    unnamed x13 -> x0, local copies, waits for them, and re-layouts: 5.07 us -> none
where the time goes in v2:
time: 69.9 us; the launch traced here: 69.8 us
  Pallas kernels  69.1 us (99%)
    pallas_call x1, Pallas kernels, body(): pl.pallas_call(functools.partial(kernel, (n, nf, exchange)), out_shape=[p...  68.1 us

profile of v2, /device:TPU:0, one launch (start us, length us, event | category | flops | bytes accessed | tf_op | source)
XLA Modules:
  0.0 69.8 jit_solution(11740904188813113636)
XLA Ops:
  0.6 68.1 %shard_map.101 = (bf16[128,512]{1,0:T(8,128)(2,1)S(1)}, bf16[128,512]{1,0:T(8,128)(2,1)S(1)}, bf16[128,1024]{1,0:T(8,128)(2,1)S(1)}, f32[512,128]{1,0:T(8,128)S(1)}, f32[512,128]{1,0:T(8,128)S(1)}) custom-call(bf16[128,512]{1,0:T(8,128)(2,1)} %refs_0_.1, bf16[128,4096]{1,0:T(8,128)(2,1)} %refs_1_.1, bf16[512,128]{1,0:T(8,128)(2,1)} %refs_2_.1, ...), custom_call_target="tpu_custom_call" | custom-call | tf_op jit(solution)/shard_map/pallas_call | solution.py:494
  68.8 1.0 %shard_map.102 = (bf16[128,512]{1,0:T(8,128)(2,1)}, bf16[128,512]{1,0:T(8,128)(2,1)}, bf16[128,1024]{1,0:T(8,128)(2,1)}, f32[512,128]{1,0:T(8,128)}, f32[512,128]{1,0:T(8,128)}) custom-call(bf16[128,512]{1,0:T(8,128)(2,1)S(1)} %get-tuple-element.10.refs_0_, bf16[128,512]{1,0:T(8,128)(2,1)S(1)} %get-tuple-element.11.refs_1_, ...), custom_call_target="tpu_custom_call" | custom-call | tf_op jit(solution)/shard_map/pallas_call | solution.py:503

commit v3 on v2

--- a/solution.py
+++ b/solution.py
@@ -94,8 +94,10 @@
     pl.semaphore_wait(barrier, n + nf - 2)
 
     class Gather:
-        def __init__(self, own, slot, send, recv):
+        def __init__(self, own, slot, send, recv, causal=False):
             self.own, self.slot, self.send, self.recv = own, slot, send, recv
+            self.give_to = outer - z if causal else outer
+            self.take_from = z + 1 if causal else outer
 
         def outgoing(self, d):
             return copy(self.own, self.slot(s), self.send.at[d], self.recv.at[s],
@@ -115,7 +117,7 @@
         def start(self):
             if inner == 2:
                 self.to_mate().start()
-            loop(1, outer, lambda d: self.outgoing(d).start())
+            loop(1, self.give_to, lambda d: self.outgoing(d).start())
 
         def forward(self):
             def step(d):
@@ -123,19 +125,19 @@
                 if inner == 2:
                     self.pass_on(d).start()
 
-            loop(1, outer, step)
+            loop(1, self.take_from, step)
 
         def finish(self):
             if inner == 2:
-                loop(0, outer, lambda d: self.arrived(
+                loop(0, self.take_from, lambda d: self.arrived(
                     (z - d + outer) % outer * inner + (inner - 1 - y)))
 
         def drain(self):
             if inner == 2:
                 self.to_mate().wait_send()
-            loop(1, outer, lambda d: self.outgoing(d).wait_send())
+            loop(1, self.give_to, lambda d: self.outgoing(d).wait_send())
             if inner == 2:
-                loop(1, outer, lambda d: self.pass_on(d).wait_send())
+                loop(1, self.take_from, lambda d: self.pass_on(d).wait_send())
 
     class Line(Gather):
         def hop(self, b, way):
@@ -196,7 +198,7 @@
     wk_gather = Line(wk_slot(s), wk_slot, wk_s, wk_r)
     wv_gather = Line(wv_slot(s), wv_slot, wv_s, wv_r)
     kv_slot = row_slot(kv_all, tok)
-    kv_gather = Gather(kv_slot(s), kv_slot, kv_s, kv_r)
+    kv_gather = Gather(kv_slot(s), kv_slot, kv_s, kv_r, causal=True)
     dkv_slot = row_slot(dkv_all, tok)
     dkv_gather = Gather(dkv_slot(s), dkv_slot, dkv_s, dkv_r)
 
@@ -395,10 +397,10 @@
     loop(1, chips, far_term)
     if cores == 2:
         join(0)
+    dkv_gather.forward()
+    dkv_gather.finish()
     if exchange:
         loop(1, nf, xf_arrived)
-    dkv_gather.forward()
-    dkv_gather.finish()
 
     total_tok = n * tok
     step = min(total_tok, 1024)

time: 69.9 us -> 68.7 us (0.983)
  Pallas kernels: 69.1 us -> 67.9 us
    pallas_call x1, Pallas kernels: 68.1 us -> 66.9 us  [body(): pl.pallas_call(functools.partial(kernel, (n, nf, exchange)), out_shape=[p...]
where the time goes in v3:
time: 68.7 us; the launch traced here: 68.6 us
  Pallas kernels  67.9 us (99%)
    pallas_call x1, Pallas kernels, body(): pl.pallas_call(functools.partial(kernel, (n, nf, exchange)), out_shape=[p...  66.9 us

profile of v3, /device:TPU:0, one launch (start us, length us, event | category | flops | bytes accessed | tf_op | source)
XLA Modules:
  0.0 68.6 jit_solution(2919036816257292482)
XLA Ops:
  0.6 66.9 %shard_map.101 = (bf16[128,512]{1,0:T(8,128)(2,1)S(1)}, bf16[128,512]{1,0:T(8,128)(2,1)S(1)}, bf16[128,1024]{1,0:T(8,128)(2,1)S(1)}, f32[512,128]{1,0:T(8,128)S(1)}, f32[512,128]{1,0:T(8,128)S(1)}) custom-call(bf16[128,512]{1,0:T(8,128)(2,1)} %refs_0_.1, bf16[128,4096]{1,0:T(8,128)(2,1)} %refs_1_.1, bf16[512,128]{1,0:T(8,128)(2,1)} %refs_2_.1, ...), custom_call_target="tpu_custom_call" | custom-call | tf_op jit(solution)/shard_map/pallas_call | solution.py:496
  67.6 1.0 %shard_map.102 = (bf16[128,512]{1,0:T(8,128)(2,1)}, bf16[128,512]{1,0:T(8,128)(2,1)}, bf16[128,1024]{1,0:T(8,128)(2,1)}, f32[512,128]{1,0:T(8,128)}, f32[512,128]{1,0:T(8,128)}) custom-call(bf16[128,512]{1,0:T(8,128)(2,1)S(1)} %get-tuple-element.10.refs_0_, bf16[128,512]{1,0:T(8,128)(2,1)S(1)} %get-tuple-element.11.refs_1_, ...), custom_call_target="tpu_custom_call" | custom-call | tf_op jit(solution)/shard_map/pallas_call | solution.py:505
